TPU v7x, 128 devices: a whole 4x4x4 slice. The times are simulated.
128 devices in a mesh: row: 8 (over y, x_lo), col: 16 (over x_hi, z, core).
Axes of the slice: x: 4 (x_hi: 2, x_lo: 2; x = x_hi * 2 + x_lo), y: 4, z: 4, core: 2. Of those that a mesh axis runs over, the one named last changes fastest.
Arguments:
- patches: bfloat16 [64, 128, 768], P('row', 'col'), may hold values from -6 to 6
- w_patch: bfloat16 [768, 6144], replicated, may hold values from -0.21875 to 0.21875
- patch_bias: bfloat16 [6144], replicated, may hold values from -5 to 5
- ln_gain: bfloat16 [6144], replicated, may hold values from 0.5 to 1.5
- w_qkv: bfloat16 [6144, 3, 48, 128], P(None, None, 'col'), may hold values from -1 to 1
- qk_gain: float32 [2, 48, 128], P(None, 'col'), may hold values from 0 to 6, as said below
- w_out: bfloat16 [48, 128, 6144], P('col', None, 'row'), may hold values from -0.078125 to 0.078125
Outputs:
- attn_branch: bfloat16 [8192, 6144], P(('row', 'col'))
Inputs may be any that keep to these rules, and one draw needn't show every extreme that they name: `qk_gain`: positive gains.
All inputs are finite; a program needn't handle non-finite values.
Results may differ from a plain program's by a relative error of at most 0.015.
Values may be sent and summed in bfloat16 or wider, within the bound.
A program may use at most 320 MiB of HBM per device.

v0:
```python
import math
import jax
import jax.numpy as jnp
from jax import lax
from jax.sharding import PartitionSpec as P

NORM_EPS = 1e-06


def sincos_table(row_ids, col_ids, model_width):
    quarter = model_width // 4
    frequency = 1.0 / 10000.0 ** (jnp.arange(quarter, dtype=jnp.float32) / quarter)
    row_angle = row_ids.astype(jnp.float32)[:, None] * frequency[None, :]
    col_angle = col_ids.astype(jnp.float32)[:, None] * frequency[None, :]
    return jnp.concatenate(
        [jnp.sin(row_angle), jnp.cos(row_angle), jnp.sin(col_angle), jnp.cos(col_angle)], axis=1
    )


def layer_norm(values, gain_row):
    mean_val = jnp.mean(values, axis=-1, keepdims=True)
    centered = values - mean_val
    variance = jnp.mean(centered * centered, axis=-1, keepdims=True)
    return centered * lax.rsqrt(variance + NORM_EPS) * gain_row


def local(patches, w_patch, patch_bias, ln_gain, w_qkv, qk_gain, w_out):
    tile_rows, tile_cols, pixel_width = patches.shape
    model_width = w_patch.shape[1]
    heads_here = w_qkv.shape[2]
    head_size = w_qkv.shape[3]
    col_count = lax.axis_size("col")
    block_tokens = tile_rows * tile_cols * col_count
    row_anchor = lax.axis_index("row") * tile_rows
    qkv_matrix = w_qkv.reshape(model_width, 3 * heads_here * head_size)
    bias_row = patch_bias.astype(jnp.float32)[None, :]
    gain_row = ln_gain.astype(jnp.float32)
    piece_cols = patches.shape[1]
    local_rows = jnp.repeat(jnp.arange(tile_rows, dtype=jnp.int32), piece_cols)
    local_cols = jnp.tile(jnp.arange(piece_cols, dtype=jnp.int32), tile_rows)
    flat_pixels = patches.reshape(tile_rows * piece_cols, pixel_width)
    embedded = jnp.dot(flat_pixels, w_patch, preferred_element_type=jnp.float32) + bias_row
    embedded = embedded + sincos_table(
        row_anchor + local_rows, lax.axis_index("col") * tile_cols + local_cols, model_width
    )
    normed = layer_norm(embedded, gain_row).astype(jnp.bfloat16)
    own_tile = normed.reshape(tile_rows, piece_cols, model_width)
    normed_piece = lax.all_gather(own_tile, "col", axis=1, tiled=True)
    piece_cols = normed_piece.shape[1]
    flat_normed = normed_piece.reshape(tile_rows * piece_cols, model_width)
    projected = jnp.dot(flat_normed, qkv_matrix, preferred_element_type=jnp.float32)
    projected = projected.reshape(tile_rows, piece_cols, 3 * heads_here * head_size)
    projected = projected.reshape(block_tokens, 3, heads_here, head_size)
    queries = layer_norm(projected[:, 0], qk_gain[0]).astype(jnp.bfloat16)
    keys_here = layer_norm(projected[:, 1], qk_gain[1]).astype(jnp.bfloat16)
    values_here = projected[:, 2].astype(jnp.bfloat16)
    query_heads = queries.transpose(1, 0, 2)
    scale_factor = 1.0 / math.sqrt(head_size)
    start_state = (
        jnp.full((heads_here, block_tokens), -1e30, jnp.float32),
        jnp.zeros((heads_here, block_tokens), jnp.float32),
        jnp.zeros((heads_here, block_tokens, head_size), jnp.float32),
    )
    key_piece = lax.all_gather(keys_here, "row", axis=0, tiled=True)
    value_piece = lax.all_gather(values_here, "row", axis=0, tiled=True)
    piece_len = key_piece.shape[0]
    key_block = math.gcd(piece_len, 1024)
    block_count = piece_len // key_block
    key_blocks = key_piece.reshape(block_count, key_block, heads_here, head_size)
    value_blocks = value_piece.reshape(block_count, key_block, heads_here, head_size)

    def step_block(state, block_args):
        run_peak, run_total, run_acc = state
        block_keys, block_values = block_args
        scores = (
            jnp.einsum("hqd,khd->hqk", query_heads, block_keys, preferred_element_type=jnp.float32)
            * scale_factor
        )
        new_peak = jnp.maximum(run_peak, jnp.max(scores, axis=2))
        rescale = jnp.exp(run_peak - new_peak)
        exponent = jnp.exp(scores - new_peak[:, :, None])
        new_total = run_total * rescale + jnp.sum(exponent, axis=2)
        weighted = jnp.einsum(
            "hqk,khd->hqd",
            exponent.astype(jnp.bfloat16),
            block_values,
            preferred_element_type=jnp.float32,
        )
        new_acc = run_acc * rescale[:, :, None] + weighted
        return ((new_peak, new_total, new_acc), None)

    final_state, unused = lax.scan(step_block, start_state, (key_blocks, value_blocks))
    peak_all, total_all, acc_all = final_state
    context = (acc_all / total_all[:, :, None]).astype(jnp.bfloat16)
    context = context.transpose(1, 0, 2).reshape(block_tokens, heads_here * head_size)
    out_weight = lax.all_gather(w_out, "row", axis=2, tiled=True).reshape(
        heads_here * head_size, model_width
    )
    return lax.psum_scatter(
        jnp.dot(context, out_weight, preferred_element_type=jnp.float32).astype(jnp.bfloat16),
        "col",
        scatter_dimension=0,
        tiled=True,
    )


def solution(mesh):
    return jax.shard_map(
        local,
        mesh=mesh,
        in_specs=(
            P("row", "col", None),
            P(),
            P(),
            P(),
            P(None, None, "col", None),
            P(None, "col", None),
            P("col", None, "row"),
        ),
        out_specs=P(("row", "col"), None),
        check_vma=False,
    )
```

profile of v0, /device:TPU:0, one launch (start us, length us, event | category | flops | bytes accessed | tf_op | source)
XLA Modules:
  0.0 726.4 jit_solution(8967606610263915652)
XLA Ops:
  7.5 2.8 multiply_sine_fusion.1
  10.3 5.6 fusion.27
  17.8 18.8 %copy.13 = bf16[6144,3,3,128]{0,3,2,1:T(8,128)(2,1)} copy(bf16[6144,3,3,128]{3,0,2,1:T(8,128)(2,1)} %param.13) | data formatting | bytes 28311552 | tf_op args[4]
  36.6 74.4 %all-gather.6.cloned.1.call-done = bf16[8,128,6144]{2,1,0:T(8,128)(2,1)} async-done(((bf16[8,8,6144]{2,1,0:T(8,128)(2,1)}), bf16[8,128,6144]{2,1,0:T(8,128)(2,1)}) %all-gather.6.cloned.1.call-update) | async-done | bytes 12582928 | tf_op jit(solution)/shard_map/all_gather | solution.py:48
  110.9 19.3 %fusion.19 = f32[1024,3,3,128]{0,3,2,1:T(8,128)S(1)} fusion(bf16[1024,6144,1,1]{1,0,3,2:T(8,128)(2,1)} %bitcast.97, bf16[6144,3,3,128]{0,3,2,1:T(8,128)(2,1)} %copy.13), kind=kOutput, calls=%fused_computation.23 | convolution fusion | flops 14495514624 | bytes 31457280 | tf_op jit(solution)/shard_map/dot_general | solution.py:51
  132.3 1.4 fusion.23
  133.8 2.4 slice.33
  138.2 122.7 %all-gather.8.cloned.1.call-done = bf16[8192,3,128]{0,2,1:T(8,128)(2,1)} async-done(((bf16[1024,3,128]{0,2,1:T(8,128)(2,1)}), bf16[8192,3,128]{0,2,1:T(8,128)(2,1)}) %all-gather.8.cloned.1.call-update) | async-done | bytes 6291472 | tf_op jit(solution)/shard_map/all_gather | solution.py:64
  260.9 12.7 %copy.21 = bf16[48,8,8,1024]{3,2,1,0:T(8,128)(2,1)} copy(bf16[48,8,8,1024]{3,1,2,0:T(8,128)(2,1)} %bitcast.95) | data formatting | bytes 12582912
  273.6 9.1 %copy.14 = bf16[8,1024,3,128]{3,1,2,0:T(8,128)(2,1)} copy(bf16[8,1024,3,128]{1,0,3,2:T(8,128)(2,1)} %bitcast.93) | data formatting | bytes 12582912
  282.8 109.8 %all-gather.12.cloned.1.call-done = bf16[8192,1,3,128]{0,3,2,1:T(8,128)(2,1)} async-done(((bf16[1024,1,3,128]{0,3,2,1:T(8,128)(2,1)}), bf16[8192,1,3,128]{0,3,2,1:T(8,128)(2,1)}) %all-gather.12.cloned.1.call-update) | async-done | bytes 6291472 | tf_op jit(solution)/shard_map/all_gather | solution.py:65
  392.6 12.7 %copy.22 = bf16[48,8,8,1024]{3,2,1,0:T(8,128)(2,1)} copy(bf16[48,8,8,1024]{3,1,2,0:T(8,128)(2,1)} %bitcast.96) | data formatting | bytes 12582912
  405.3 9.2 %copy.16 = bf16[8,1024,3,128]{3,1,2,0:T(8,128)(2,1)} copy(bf16[8,1024,3,128]{1,0,3,2:T(8,128)(2,1)} %bitcast.94) | data formatting | bytes 12582912
  414.5 170.3 %while.15 = (s32[]{:T(128)}, f32[3,1024]{1,0:T(4,128)S(1)}, f32[3,1024]{1,0:T(4,128)S(1)}, f32[3,1024,128]{2,1,0:T(8,128)}, bf16[8,1024,3,128]{3,1,2,0:T(8,128)(...) while((s32[]{:T(128)}, f32[3,1024]{1,0:T(4,128)S(1)}, ...), condition=%wide.region_9.10_spmd.clone, body=%wide.region_6.9_spmd.clone.sunk | while | flops 1636973568 | bytes 93783168 | solution.py:92
  414.5 7.7 %bitcast_reduce_fusion.2 = (f32[3,1024]{1,0:T(4,128)S(1)}, f32[3,1024,1024]{2,1,0:T(8,128)}) fusion(bf16[3,1024,128]{2,1,0:T(8,128)(2,1)} %get-tuple-element.195, bf16[8,1024,3,128]{3,1,2,0:T(8,128)(2,1)} %get-tuple-element.194, s32[]{:T(128)} %get-tuple-element.181), kind=kOutput, calls=%fused_computation.1.clone.1 | convolution fusion | flops 811594752 | bytes 14168576 | tf_op jit(solution)/shard_map/while/body/eval_jaxpr/hqd,khd->hqk/dot_general | solution.py:76
  422.3 6.9 fusion.41
  429.2 1.4 copy-done.2
  430.6 5.1 fusion.43
  435.7 7.7 %bitcast_reduce_fusion.2 = (f32[3,1024]{1,0:T(4,128)S(1)}, f32[3,1024,1024]{2,1,0:T(8,128)}) fusion(bf16[3,1024,128]{2,1,0:T(8,128)(2,1)} %get-tuple-element.195, bf16[8,1024,3,128]{3,1,2,0:T(8,128)(2,1)} %get-tuple-element.194, s32[]{:T(128)} %get-tuple-element.181), kind=kOutput, calls=%fused_computation.1.clone.1 | convolution fusion | flops 811594752 | bytes 14168576 | tf_op jit(solution)/shard_map/while/body/eval_jaxpr/hqd,khd->hqk/dot_general | solution.py:76
  443.5 6.8 fusion.41
  450.3 1.4 copy-done.2
  451.7 5.4 fusion.43
  457.1 7.8 %bitcast_reduce_fusion.2 = (f32[3,1024]{1,0:T(4,128)S(1)}, f32[3,1024,1024]{2,1,0:T(8,128)}) fusion(bf16[3,1024,128]{2,1,0:T(8,128)(2,1)} %get-tuple-element.195, bf16[8,1024,3,128]{3,1,2,0:T(8,128)(2,1)} %get-tuple-element.194, s32[]{:T(128)} %get-tuple-element.181), kind=kOutput, calls=%fused_computation.1.clone.1 | convolution fusion | flops 811594752 | bytes 14168576 | tf_op jit(solution)/shard_map/while/body/eval_jaxpr/hqd,khd->hqk/dot_general | solution.py:76
  464.9 6.8 fusion.41
  471.7 1.4 copy-done.2
  473.1 5.4 fusion.43
  478.5 7.7 %bitcast_reduce_fusion.2 = (f32[3,1024]{1,0:T(4,128)S(1)}, f32[3,1024,1024]{2,1,0:T(8,128)}) fusion(bf16[3,1024,128]{2,1,0:T(8,128)(2,1)} %get-tuple-element.195, bf16[8,1024,3,128]{3,1,2,0:T(8,128)(2,1)} %get-tuple-element.194, s32[]{:T(128)} %get-tuple-element.181), kind=kOutput, calls=%fused_computation.1.clone.1 | convolution fusion | flops 811594752 | bytes 14168576 | tf_op jit(solution)/shard_map/while/body/eval_jaxpr/hqd,khd->hqk/dot_general | solution.py:76
  486.3 6.8 fusion.41
  493.1 1.3 copy-done.2
  494.4 5.4 fusion.43
  499.8 7.7 %bitcast_reduce_fusion.2 = (f32[3,1024]{1,0:T(4,128)S(1)}, f32[3,1024,1024]{2,1,0:T(8,128)}) fusion(bf16[3,1024,128]{2,1,0:T(8,128)(2,1)} %get-tuple-element.195, bf16[8,1024,3,128]{3,1,2,0:T(8,128)(2,1)} %get-tuple-element.194, s32[]{:T(128)} %get-tuple-element.181), kind=kOutput, calls=%fused_computation.1.clone.1 | convolution fusion | flops 811594752 | bytes 14168576 | tf_op jit(solution)/shard_map/while/body/eval_jaxpr/hqd,khd->hqk/dot_general | solution.py:76
  507.5 6.8 fusion.41
  514.4 1.3 copy-done.2
  515.7 5.4 fusion.43
  521.0 7.7 %bitcast_reduce_fusion.2 = (f32[3,1024]{1,0:T(4,128)S(1)}, f32[3,1024,1024]{2,1,0:T(8,128)}) fusion(bf16[3,1024,128]{2,1,0:T(8,128)(2,1)} %get-tuple-element.195, bf16[8,1024,3,128]{3,1,2,0:T(8,128)(2,1)} %get-tuple-element.194, s32[]{:T(128)} %get-tuple-element.181), kind=kOutput, calls=%fused_computation.1.clone.1 | convolution fusion | flops 811594752 | bytes 14168576 | tf_op jit(solution)/shard_map/while/body/eval_jaxpr/hqd,khd->hqk/dot_general | solution.py:76
  528.8 6.8 fusion.41
  535.6 1.3 copy-done.2
  537.0 5.4 fusion.43
  542.3 7.7 %bitcast_reduce_fusion.2 = (f32[3,1024]{1,0:T(4,128)S(1)}, f32[3,1024,1024]{2,1,0:T(8,128)}) fusion(bf16[3,1024,128]{2,1,0:T(8,128)(2,1)} %get-tuple-element.195, bf16[8,1024,3,128]{3,1,2,0:T(8,128)(2,1)} %get-tuple-element.194, s32[]{:T(128)} %get-tuple-element.181), kind=kOutput, calls=%fused_computation.1.clone.1 | convolution fusion | flops 811594752 | bytes 14168576 | tf_op jit(solution)/shard_map/while/body/eval_jaxpr/hqd,khd->hqk/dot_general | solution.py:76
  550.1 6.8 fusion.41
  556.9 1.3 copy-done.2
  558.2 5.4 fusion.43
  563.6 7.7 %bitcast_reduce_fusion.2 = (f32[3,1024]{1,0:T(4,128)S(1)}, f32[3,1024,1024]{2,1,0:T(8,128)}) fusion(bf16[3,1024,128]{2,1,0:T(8,128)(2,1)} %get-tuple-element.195, bf16[8,1024,3,128]{3,1,2,0:T(8,128)(2,1)} %get-tuple-element.194, s32[]{:T(128)} %get-tuple-element.181), kind=kOutput, calls=%fused_computation.1.clone.1 | convolution fusion | flops 811594752 | bytes 14168576 | tf_op jit(solution)/shard_map/while/body/eval_jaxpr/hqd,khd->hqk/dot_general | solution.py:76
  571.4 6.8 fusion.41
  578.2 1.3 copy-done.2
  579.5 5.4 fusion.43
  584.9 11.9 %bitcast_convert_fusion = bf16[1024,6144]{1,0:T(8,128)(2,1)} fusion(bf16[3,128,6144]{2,1,0:T(8,128)(2,1)} %all-gather.10.cloned.1.call-done, f32[3,1024,128]{2,1,0:T(8,128)} %get-tuple-element.43, f32[3,1024]{1,0:T(4,128)S(1)} %get-tuple-element.44), kind=kOutput, calls=%fused_computation.22 | convolution fusion | flops 4838916096 | bytes 18886656 | tf_op jit(solution)/shard_map/dot_general | solution.py:100
  596.8 123.1 %reduce-scatter.2.cloned.1.call-done = bf16[64,6144]{1,0:T(8,128)(2,1)} async-done(((bf16[1024,6144]{1,0:T(8,128)(2,1)}), bf16[64,6144]{1,0:T(8,128)(2,1)}) %reduce-scatter.2.cloned.1.call-update) | async-done | bytes 786448 | tf_op jit(solution)/shard_map/reduce_scatter | solution.py:99
  (75 shorter events, 7.3 us)
Async XLA Ops:
  6.5 3.7 copy-start
  6.5 104.4 %all-gather.6.cloned.1.call-start = ((), (), s32[]{:S(2)}) async-start(), calls=%async_computation.1 | async-start | bytes 13369344 | tf_op jit(solution)/shard_map/all_gather | solution.py:48
  15.8 0.7 copy-start.4
  17.7 18.9 %copy-start.5 = (f32[2,3,128]{2,0,1:T(2,128)S(1)}, f32[2,3,128]{2,0,1:T(2,128)}, u32[]{:S(2)}) copy-start(f32[2,3,128]{2,0,1:T(2,128)} %param.14) | copy-start | bytes 9220
  17.7 243.2 %all-gather.8.cloned.1.call-start = ((), (), s32[]{:S(2)}) async-start(), calls=%async_computation.2 | async-start | bytes 7077888 | tf_op jit(solution)/shard_map/all_gather | solution.py:64
  130.2 2.1 copy-start.3
  133.7 258.8 %all-gather.12.cloned.1.call-start = ((), (), s32[]{:S(2)}) async-start(), calls=%async_computation.5 | async-start | bytes 7077888 | tf_op jit(solution)/shard_map/all_gather | solution.py:65
  136.2 448.6 %all-gather.10.cloned.1.call-start = ((), (), s32[]{:S(2)}) async-start(), calls=%async_computation.3 | async-start | bytes 5308416 | tf_op jit(solution)/shard_map/all_gather | solution.py:96
  136.8 583.1 %reduce-scatter.2.cloned.1.call-start = ((), (), s32[]{:S(2)}) async-start(), calls=%async_computation.4 | async-start | bytes 13369344 | tf_op jit(solution)/shard_map/reduce_scatter | solution.py:99
  422.3 8.3 %copy-start.2 = (f32[3,1024,1024]{2,1,0:T(8,128)S(1)}, f32[3,1024,1024]{2,1,0:T(8,128)}, u32[]{:S(2)}) copy-start(f32[3,1024,1024]{2,1,0:T(8,128)} %get-tuple-element.169) | copy-start | bytes 37748740 | tf_op jit(solution)/shard_map/while
  443.5 8.3 %copy-start.2 = (f32[3,1024,1024]{2,1,0:T(8,128)S(1)}, f32[3,1024,1024]{2,1,0:T(8,128)}, u32[]{:S(2)}) copy-start(f32[3,1024,1024]{2,1,0:T(8,128)} %get-tuple-element.169) | copy-start | bytes 37748740 | tf_op jit(solution)/shard_map/while
  464.9 8.3 %copy-start.2 = (f32[3,1024,1024]{2,1,0:T(8,128)S(1)}, f32[3,1024,1024]{2,1,0:T(8,128)}, u32[]{:S(2)}) copy-start(f32[3,1024,1024]{2,1,0:T(8,128)} %get-tuple-element.169) | copy-start | bytes 37748740 | tf_op jit(solution)/shard_map/while
  486.3 8.2 %copy-start.2 = (f32[3,1024,1024]{2,1,0:T(8,128)S(1)}, f32[3,1024,1024]{2,1,0:T(8,128)}, u32[]{:S(2)}) copy-start(f32[3,1024,1024]{2,1,0:T(8,128)} %get-tuple-element.169) | copy-start | bytes 37748740 | tf_op jit(solution)/shard_map/while
  507.5 8.2 %copy-start.2 = (f32[3,1024,1024]{2,1,0:T(8,128)S(1)}, f32[3,1024,1024]{2,1,0:T(8,128)}, u32[]{:S(2)}) copy-start(f32[3,1024,1024]{2,1,0:T(8,128)} %get-tuple-element.169) | copy-start | bytes 37748740 | tf_op jit(solution)/shard_map/while
  528.8 8.2 %copy-start.2 = (f32[3,1024,1024]{2,1,0:T(8,128)S(1)}, f32[3,1024,1024]{2,1,0:T(8,128)}, u32[]{:S(2)}) copy-start(f32[3,1024,1024]{2,1,0:T(8,128)} %get-tuple-element.169) | copy-start | bytes 37748740 | tf_op jit(solution)/shard_map/while
  550.1 8.2 %copy-start.2 = (f32[3,1024,1024]{2,1,0:T(8,128)S(1)}, f32[3,1024,1024]{2,1,0:T(8,128)}, u32[]{:S(2)}) copy-start(f32[3,1024,1024]{2,1,0:T(8,128)} %get-tuple-element.169) | copy-start | bytes 37748740 | tf_op jit(solution)/shard_map/while
  571.3 8.2 %copy-start.2 = (f32[3,1024,1024]{2,1,0:T(8,128)S(1)}, f32[3,1024,1024]{2,1,0:T(8,128)}, u32[]{:S(2)}) copy-start(f32[3,1024,1024]{2,1,0:T(8,128)} %get-tuple-element.169) | copy-start | bytes 37748740 | tf_op jit(solution)/shard_map/while
  596.8 123.1 %copy-start.1 = (bf16[8,8,768]{2,1,0:T(8,128)(2,1)S(1)}, bf16[8,8,768]{2,1,0:T(8,128)(2,1)}, u32[]{:S(2)}) copy-start(bf16[8,8,768]{2,1,0:T(8,128)(2,1)} %param.9) | copy-start | bytes 294916
Sparse Core Ops, SparseCore 0:
  17.8 93.0 all-gather.5
  133.9 127.0 all-gather.7
  262.6 129.9 all-gather.11
  394.1 100.9 all-gather.9
  596.9 122.9 reduce-scatter.1
where the time goes:
time: 728 us; the launch traced here: 726 us
  waiting for transfers between devices  431 us (59%)
  matrix products  141 us (19%)
  local copies, waits for them, and re-layouts  78.8 us (11%)
  other arithmetic  61.9 us (9%)
  between operations  13.3 us (2%)
    reduce_scatter x1, waiting for transfers between devices, local(): lax.psum_scatter(jnp.dot(context, out_weight, preferred_element_type=jnp....  123 us
    all_gather x1, waiting for transfers between devices, local(): key_piece = lax.all_gather(keys_here, 'row', axis=0, tiled=True)  123 us
    all_gather x1, waiting for transfers between devices, local(): value_piece = lax.all_gather(values_here, 'row', axis=0, tiled=True)  110 us
    all_gather x1, waiting for transfers between devices, local(): normed_piece = lax.all_gather(own_tile, 'col', axis=1, tiled=True)  74.4 us
    unnamed x17, local copies, waits for them, and re-layouts  65.4 us
    dot_general x8, matrix products, step_block(): jnp.einsum('hqd,khd->hqk', query_heads, block_keys, preferred_element_typ...  62 us
    reduce_sum x8, other arithmetic, step_block(): new_total = run_total * rescale + jnp.sum(exponent, axis=2)  54.5 us
    dot_general x8, matrix products, step_block(): jnp.einsum('hqk,khd->hqd', exponent.astype(jnp.bfloat16), block_values, p...  42.6 us
  transfers between devices with their start and end apart: 5, of which 4 were waited for; matrix products, arithmetic and copies ran while one was open for 31% of the time, Pallas kernels for 0%

commit v1 on v0

--- a/solution.py
+++ b/solution.py
@@ -45,7 +45,8 @@
     )
     normed = layer_norm(embedded, gain_row).astype(jnp.bfloat16)
     own_tile = normed.reshape(tile_rows, piece_cols, model_width)
-    normed_piece = lax.all_gather(own_tile, "col", axis=1, tiled=True)
+    outgoing = jnp.stack([own_tile] * lax.axis_size("col"))
+    normed_piece = jnp.concatenate(lax.all_to_all(outgoing, "col", 0, 0), axis=1)
     piece_cols = normed_piece.shape[1]
     flat_normed = normed_piece.reshape(tile_rows * piece_cols, model_width)
     projected = jnp.dot(flat_normed, qkv_matrix, preferred_element_type=jnp.float32)

time: 728 us -> 865 us (1.19)
  waiting for transfers between devices: 431 us -> 535 us
  local copies, waits for them, and re-layouts: 78.8 us -> 98.2 us
  starting transfers between devices: 0.35 us -> 9.01 us
    all_to_all x0 -> x1, waiting for transfers between devices: none -> 168 us  [local(): lax.all_to_all(outgoing, 'col', 0, 0)]
    all_gather x1 -> x0, waiting for transfers between devices: 74.4 us -> none  [local(): normed_piece = lax.all_gather(own_tile, 'col', axis=1, tiled=True)]
    reshape x0 -> x1, local copies, waits for them, and re-layouts: none -> 11.4 us  [local(): jnp.concatenate(lax.all_to_all(outgoing, 'col', 0, 0), axis=1)]
    all_gather x1, waiting for transfers between devices: 123 us -> 133 us  [local(): key_piece = lax.all_gather(keys_here, 'row', axis=0, tiled=True)]
    unnamed x17 -> x19, local copies, waits for them, and re-layouts: 65.4 us -> 67.2 us
  transfers between devices with their start and end apart: 5 -> 5, of which waited for: 4 -> 4; matrix products, arithmetic and copies ran while one was open for 31% -> 26% of each run, Pallas kernels for 0% -> 0%
where the time goes in v1:
time: 865 us; the launch traced here: 859 us
  waiting for transfers between devices  535 us (62%)
  matrix products  142 us (16%)
  local copies, waits for them, and re-layouts  98.2 us (11%)
  other arithmetic  61 us (7%)
  between operations  13.5 us (2%)
  starting transfers between devices  9.01 us (1%)
    all_to_all x1, waiting for transfers between devices, local(): lax.all_to_all(outgoing, 'col', 0, 0)  168 us
    all_gather x1, waiting for transfers between devices, local(): key_piece = lax.all_gather(keys_here, 'row', axis=0, tiled=True)  133 us
    reduce_scatter x1, waiting for transfers between devices, local(): lax.psum_scatter(jnp.dot(context, out_weight, preferred_element_type=jnp....  123 us
    all_gather x1, waiting for transfers between devices, local(): value_piece = lax.all_gather(values_here, 'row', axis=0, tiled=True)  110 us
    unnamed x19, local copies, waits for them, and re-layouts  67.2 us
    dot_general x8, matrix products, step_block(): jnp.einsum('hqd,khd->hqk', query_heads, block_keys, preferred_element_typ...  61.7 us
    reduce_sum x8, other arithmetic, step_block(): new_total = run_total * rescale + jnp.sum(exponent, axis=2)  54.5 us
    dot_general x8, matrix products, step_block(): jnp.einsum('hqk,khd->hqd', exponent.astype(jnp.bfloat16), block_values, p...  42.6 us
  transfers between devices with their start and end apart: 5, of which 4 were waited for; matrix products, arithmetic and copies ran while one was open for 26% of the time, Pallas kernels for 0%

profile of v1, /device:TPU:0, one launch (start us, length us, event | category | flops | bytes accessed | tf_op | source)
XLA Modules:
  0.0 858.8 jit_solution(1056067448675297207)
XLA Ops:
  7.4 2.8 multiply_sine_fusion.1
  10.2 5.6 fusion.27
  16.8 6.1 stack.3
  22.9 8.0 all-to-all-start
  31.3 18.7 %copy.19 = bf16[6144,3,3,128]{0,3,2,1:T(8,128)(2,1)} copy(bf16[6144,3,3,128]{3,0,2,1:T(8,128)(2,1)} %param.13) | data formatting | bytes 28311552 | tf_op args[4]
  50.0 168.5 %all-to-all-done = bf16[16,8,8,6144]{3,2,1,0:T(8,128)(2,1)} async-done(((bf16[16,8,8,6144]{3,2,1,0:T(8,128)(2,1)}), bf16[16,8,8,6144]{3,2,1,0:T(8,128)(2,1)}, u32[]{:S(2)}, u32[]{:S(2)}) %all-to-all-start) | async-done | bytes 12582944 | tf_op jit(solution)/shard_map/all_to_all | solution.py:49
  218.5 11.4 %copy.18 = bf16[8,16,8,6144]{3,2,1,0:T(8,128)(2,1)} copy(bf16[8,16,8,6144]{3,2,0,1:T(8,128)(2,1)} %bitcast.2) | data formatting | bytes 25165824 | tf_op jit(solution)/shard_map/reshape | solution.py:49
  229.9 2.0 copy-done.4
  231.9 20.3 %fusion.19 = f32[1024,3,3,128]{0,3,2,1:T(8,128)S(1)} fusion(bf16[1024,6144,1,1]{1,0,3,2:T(8,128)(2,1)} %bitcast.96, bf16[6144,3,3,128]{0,3,2,1:T(8,128)(2,1)S(1)} %copy-done.4), kind=kOutput, calls=%fused_computation.23 | convolution fusion | flops 14495514624 | bytes 31457280 | tf_op jit(solution)/shard_map/dot_general | solution.py:52
  254.4 1.4 fusion.23
  255.8 2.4 slice.33
  260.7 132.7 %all-gather.5.cloned.1.call-done = bf16[8192,3,128]{0,2,1:T(8,128)(2,1)} async-done(((bf16[1024,3,128]{0,2,1:T(8,128)(2,1)}), bf16[8192,3,128]{0,2,1:T(8,128)(2,1)}) %all-gather.5.cloned.1.call-update) | async-done | bytes 6291472 | tf_op jit(solution)/shard_map/all_gather | solution.py:65
  393.4 12.6 %copy.27 = bf16[48,8,8,1024]{3,2,1,0:T(8,128)(2,1)} copy(bf16[48,8,8,1024]{3,1,2,0:T(8,128)(2,1)} %bitcast.97) | data formatting | bytes 12582912
  406.1 9.3 %copy.20 = bf16[8,1024,3,128]{3,1,2,0:T(8,128)(2,1)} copy(bf16[8,1024,3,128]{1,0,3,2:T(8,128)(2,1)} %bitcast.94) | data formatting | bytes 12582912
  415.3 109.7 %all-gather.9.cloned.1.call-done = bf16[8192,1,3,128]{0,3,2,1:T(8,128)(2,1)} async-done(((bf16[1024,1,3,128]{0,3,2,1:T(8,128)(2,1)}), bf16[8192,1,3,128]{0,3,2,1:T(8,128)(2,1)}) %all-gather.9.cloned.1.call-update) | async-done | bytes 6291472 | tf_op jit(solution)/shard_map/all_gather | solution.py:66
  525.0 12.7 %copy.28 = bf16[48,8,8,1024]{3,2,1,0:T(8,128)(2,1)} copy(bf16[48,8,8,1024]{3,1,2,0:T(8,128)(2,1)} %bitcast.98) | data formatting | bytes 12582912
  537.7 9.1 %copy.22 = bf16[8,1024,3,128]{3,1,2,0:T(8,128)(2,1)} copy(bf16[8,1024,3,128]{1,0,3,2:T(8,128)(2,1)} %bitcast.95) | data formatting | bytes 12582912
  546.8 170.2 %while.15 = (s32[]{:T(128)}, f32[3,1024]{1,0:T(4,128)S(1)}, f32[3,1024]{1,0:T(4,128)S(1)}, f32[3,1024,128]{2,1,0:T(8,128)}, bf16[8,1024,3,128]{3,1,2,0:T(8,128)(...) while((s32[]{:T(128)}, f32[3,1024]{1,0:T(4,128)S(1)}, ...), condition=%wide.region_9.10_spmd.clone, body=%wide.region_6.9_spmd.clone.sunk | while | flops 1636973568 | bytes 93783168 | solution.py:93
  547.0 7.7 bitcast_reduce_fusion.2
  554.8 6.9 fusion.41
  561.7 1.4 copy-done.2
  563.1 5.1 fusion.43
  568.2 7.7 bitcast_reduce_fusion.2
  575.9 6.8 fusion.41
  582.8 1.4 copy-done.2
  584.2 5.3 fusion.43
  589.5 7.7 bitcast_reduce_fusion.2
  597.3 6.8 fusion.41
  604.1 1.4 copy-done.2
  605.5 5.4 fusion.43
  610.9 7.7 bitcast_reduce_fusion.2
  618.6 6.8 fusion.41
  625.4 1.3 copy-done.2
  626.8 5.3 fusion.43
  632.1 7.7 bitcast_reduce_fusion.2
  639.9 6.8 fusion.41
  648.0 5.3 fusion.43
  653.4 7.7 bitcast_reduce_fusion.2
  661.1 6.8 fusion.41
  669.2 5.3 fusion.43
  674.6 7.7 bitcast_reduce_fusion.2
  682.3 6.8 fusion.41
  690.5 5.3 fusion.43
  695.8 7.7 bitcast_reduce_fusion.2
  703.6 6.8 fusion.41
  711.7 5.3 fusion.43
  717.1 11.8 %bitcast_convert_fusion = bf16[1024,6144]{1,0:T(8,128)(2,1)} fusion(bf16[3,128,6144]{2,1,0:T(8,128)(2,1)} %all-gather.7.cloned.1.call-done, f32[3,1024,128]{2,1,0:T(8,128)} %get-tuple-element.43, f32[3,1024]{1,0:T(4,128)S(1)} %get-tuple-element.44), kind=kOutput, calls=%fused_computation.22 | convolution fusion | flops 4838916096 | bytes 18886656 | tf_op jit(solution)/shard_map/dot_general | solution.py:101
  728.9 123.1 %reduce-scatter.2.cloned.1.call-done = bf16[64,6144]{1,0:T(8,128)(2,1)} async-done(((bf16[1024,6144]{1,0:T(8,128)(2,1)}), bf16[64,6144]{1,0:T(8,128)(2,1)}) %reduce-scatter.2.cloned.1.call-update) | async-done | bytes 786448 | tf_op jit(solution)/shard_map/reduce_scatter | solution.py:100
  (78 shorter events, 12.5 us)
Async XLA Ops:
  6.5 3.7 copy-start
  15.8 0.7 copy-start.5
  22.9 195.6 %all-to-all-start = ((bf16[16,8,8,6144]{3,2,1,0:T(8,128)(2,1)}), bf16[16,8,8,6144]{3,2,1,0:T(8,128)(2,1)}, u32[]{:S(2)}, u32[]{:S(2)}) async-start(bf16[16,8,8,6144]{3,2,1,0:T(8,128)(2,1)} %stack.3), calls=%async_computation | async-start | bytes 25165824 | tf_op jit(solution)/shard_map/all_to_all | solution.py:49
  31.0 19.1 %copy-start.6 = (f32[2,3,128]{2,0,1:T(2,128)S(1)}, f32[2,3,128]{2,0,1:T(2,128)}, u32[]{:S(2)}) copy-start(f32[2,3,128]{2,0,1:T(2,128)} %param.14) | copy-start | bytes 9220
  31.0 362.4 %all-gather.5.cloned.1.call-start = ((), (), s32[]{:S(2)}) async-start(), calls=%async_computation.2 | async-start | bytes 7077888 | tf_op jit(solution)/shard_map/all_gather | solution.py:65
  218.5 13.4 %copy-start.4 = (bf16[6144,3,3,128]{0,3,2,1:T(8,128)(2,1)S(1)}, bf16[6144,3,3,128]{0,3,2,1:T(8,128)(2,1)}, u32[]{:S(2)}) copy-start(bf16[6144,3,3,128]{0,3,2,1:T(8,128)(2,1)} %copy.19) | copy-start | bytes 42467332
  252.2 2.1 copy-start.3
  255.8 269.3 %all-gather.9.cloned.1.call-start = ((), (), s32[]{:S(2)}) async-start(), calls=%async_computation.5 | async-start | bytes 7077888 | tf_op jit(solution)/shard_map/all_gather | solution.py:66
  258.2 458.8 %all-gather.7.cloned.1.call-start = ((), (), s32[]{:S(2)}) async-start(), calls=%async_computation.3 | async-start | bytes 5308416 | tf_op jit(solution)/shard_map/all_gather | solution.py:97
  259.0 593.1 %reduce-scatter.2.cloned.1.call-start = ((), (), s32[]{:S(2)}) async-start(), calls=%async_computation.4 | async-start | bytes 13369344 | tf_op jit(solution)/shard_map/reduce_scatter | solution.py:100
  554.8 8.3 copy-start.2
  575.9 8.3 copy-start.2
  597.3 8.3 copy-start.2
  618.6 8.2 copy-start.2
  639.9 8.2 copy-start.2
  661.1 8.2 copy-start.2
  682.3 8.2 copy-start.2
  703.5 8.2 copy-start.2
  728.9 123.1 %copy-start.1 = (bf16[8,8,768]{2,1,0:T(8,128)(2,1)S(1)}, bf16[8,8,768]{2,1,0:T(8,128)(2,1)}, u32[]{:S(2)}) copy-start(bf16[8,8,768]{2,1,0:T(8,128)(2,1)} %param.9) | copy-start | bytes 294916
Sparse Core Ops, SparseCore 0:
  255.9 137.4 all-gather.4
  395.1 129.9 all-gather.8
  526.7 100.9 all-gather.6
  729.0 122.9 reduce-scatter.1
